TPU v7x, 256 devices: a whole 4x4x8 slice. The times are simulated.
256 devices in a mesh: row: 16 (over z, core), col: 16 (over x, y).
Axes of the slice: x: 4, y: 4, z: 8, core: 2. Of those that a mesh axis runs over, the one named last changes fastest.
Arguments:
- genotypes: int32 [4096, 16384], P(('row', 'col')), may hold values from 0 to 2, as said below
- snp_index: int32 [4096], P(('row', 'col')), may hold values from 0 to 16383, as said below
- freq_table: float32 [16384], replicated, as said below
- prior: float32 [16384, 16384], P('row', 'col'), as said below
- start_vectors: float32 [16384, 20], P('row'), may hold values from -6 to 6
Outputs:
- grm: float32 [16384, 16384], P('row', 'col')
- pcs: float32 [16384, 20], P('col')
- spectrum: float32 [3, 20], replicated
Inputs may be any that keep to these rules, and one draw needn't show every extreme that they name: `genotypes`: genotype dosages 0, 1 or 2. `snp_index`: strictly increasing; entry j lies in 4 * j to 4 * j + 3. `freq_table`: frequencies are multiples of 1/1024 between 52/1024 and 512/1024. `prior`: exactly symmetric; diagonal between 1 and 2, off-diagonal entries small.
All inputs are finite; a program needn't handle non-finite values.
Results may differ from a plain program's by a relative error of at most 0.0075.
Values may be sent and summed in bfloat16 or wider, within the bound.
No kernel may reach another device: no remote copies, remote signals or barrier semaphores. Data moves between devices by JAX's collectives and lax.ppermute only.
A program may use at most 128 MiB of HBM per device.

v0:
```python
import jax
import jax.numpy as jnp
from jax import lax
from jax.sharding import Mesh
from jax.sharding import PartitionSpec as P

S = 16384
ITERS = 3
COL = ("col_0", "col_1")
ROW_COL = ("row", "col_0", "col_1")


def total_of_pieces(array, axis):
    return lax.all_gather(array, axis).sum(0)


def copy_for_each(array, axis):
    length = lax.axis_size(axis)
    return lax.all_to_all(
        jnp.broadcast_to(array[None], (length, *array.shape)), axis, 0, 0, tiled=True
    )


def taken_together(array, axis):
    return copy_for_each(array, axis).sum(axis=0)


def in_one(arrays, axis):
    ravelled, at, outs = (jnp.concatenate([a.reshape(-1) for a in arrays]), 0, [])
    so_far = taken_together(ravelled, axis)
    for a in arrays:
        outs.append(so_far[at : at + a.size].reshape(a.shape))
        at += a.size
    return tuple(outs)


def one_axis_at_a_time(array, axes):
    for axis in axes:
        array = lax.psum(array, axis)
    return array


def standardize(genotypes, allele_freq):
    doubled = 2.0 * allele_freq
    spread = jnp.sqrt(doubled * (1.0 - allele_freq))
    return (genotypes.astype(jnp.float32) - doubled[:, None]) / spread[:, None]


def orthonormal(factor, image):
    return lax.linalg.triangular_solve(factor, image, left_side=False, lower=True, transpose_a=True)


def apply_tile(tile, vectors, transposed):
    if transposed:
        return lax.dot_general(tile, vectors, (((0,), (0,)), ((), ())))
    return jnp.dot(tile, vectors)


def local_gram(image):
    return jnp.dot(image.T, image)


def body(genotypes, snp_index, freq_table, prior, start_vectors):
    allele_freq = jnp.take(freq_table, snp_index)
    standard = standardize(genotypes, allele_freq).astype(jnp.bfloat16)
    row_count = lax.axis_size("row")
    col_count = lax.axis_size(COL)
    own_snps = genotypes.shape[0]
    total_snps = own_snps * row_count * col_count
    row_piece = lax.all_to_all(standard, "row", split_axis=1, concat_axis=0, tiled=True)
    col_piece = lax.all_to_all(standard, COL, split_axis=1, concat_axis=0, tiled=True)
    col_piece = col_piece.reshape(col_count, 1, own_snps, col_piece.shape[1])
    col_panel = lax.all_gather(col_piece, "row", axis=1, tiled=True)
    col_panel = col_panel.reshape(total_snps, col_panel.shape[3])
    window = lax.dot_general(
        lax.all_gather(row_piece, COL, axis=0, tiled=True),
        col_panel,
        (((0,), (0,)), ((), ())),
        preferred_element_type=jnp.float32,
    )
    grm = prior + window / total_snps
    scaled_start = start_vectors / jnp.sqrt(jnp.float32(S))
    diagonals = []
    image = total_of_pieces(apply_tile(grm, scaled_start, True), "row")
    for step in range(1, ITERS):
        if step % 2 == 1:
            product, gram = in_one((apply_tile(grm, image, False), local_gram(image)), COL)
        else:
            product, gram = (
                total_of_pieces(apply_tile(grm, image, True), "row"),
                total_of_pieces(local_gram(image), "row"),
            )
        factor = jnp.linalg.cholesky(gram)
        diagonals.append(jnp.diagonal(factor))
        image = orthonormal(factor, product)
    gram = one_axis_at_a_time(local_gram(image), COL)
    factor = jnp.linalg.cholesky(gram)
    diagonals.append(jnp.diagonal(factor))
    vectors = orthonormal(factor, image)
    pcs = vectors * jnp.sqrt(jnp.float32(S))
    spectrum = jnp.stack(diagonals, axis=0)
    return (grm, pcs, spectrum)


def solution(mesh):
    finer = Mesh(mesh.devices.reshape(mesh.shape["row"], 4, 4), ("row", "col_0", "col_1"))
    in_specs = (P(ROW_COL, None), P(ROW_COL), P(), P("row", COL), P("row", None))
    out_specs = (P("row", COL), P(COL, None), P())
    return jax.shard_map(body, mesh=finer, in_specs=in_specs, out_specs=out_specs, check_vma=False)
```

profile of v0, /device:TPU:32, one launch (start us, length us, event | category | flops | bytes accessed | tf_op | source)
XLA Modules:
  0.0 351.4 jit_solution(14662210511644327606)
XLA Ops:
  7.2 0.7 compare_select_fusion
  8.0 0.7 gather_fusion
  8.7 0.7 broadcast_multiply_fusion
  9.3 1.4 divide_convert_fusion
  10.8 18.3 %all_to_all.38 = bf16[16,16,1024]{2,0,1:T(8,128)(2,1)S(1)} all-to-all(bf16[16,16,1024]{2,0,1:T(8,128)(2,1)S(1)} %bitcast.82), channel_id=1, replica_groups=mesh['row'=16,'col_0'=4,'col_1'=4] {'col_0','col_1'}, dimensions={1} | all-to-all | bytes 1048576 | tf_op jit(solution)/shard_map/all_to_all | solution.py:71
  29.1 1.1 copy.44
  30.3 25.6 %all_to_all.39 = bf16[16,16,1024]{2,0,1:T(8,128)(2,1)} all-to-all(bf16[16,16,1024]{2,0,1:T(8,128)(2,1)S(1)} %bitcast.83), channel_id=1, replica_groups=mesh['row'=16,'col_0'=4,'col_1'=4] {'row'}, dimensions={1} | all-to-all | bytes 1048576 | tf_op jit(solution)/shard_map/all_to_all | solution.py:70
  55.9 37.5 %all-gather.12.cloned.1.call-done = bf16[16,256,1024]{2,0,1:T(8,128)(2,1)} async-done(((bf16[16,16,1024]{2,0,1:T(8,128)(2,1)}), bf16[16,256,1024]{2,0,1:T(8,128)(2,1)}) %all-gather.12.cloned.1.call-update) | async-done | bytes 8388624 | tf_op jit(solution)/shard_map/all_gather | solution.py:73
  93.5 11.3 %copy.45 = bf16[16,256,1024]{2,1,0:T(8,128)(2,1)} copy(bf16[16,256,1024]{2,0,1:T(8,128)(2,1)} %all-gather.12.cloned.1.call-done) | data formatting | bytes 16777216 | tf_op jit(solution)/shard_map/all_gather | solution.py:73
  104.8 63.9 %all-gather.10.cloned.1.call-done = bf16[4096,1024]{1,0:T(8,128)(2,1)} async-done(((bf16[256,1024]{1,0:T(8,128)(2,1)}), bf16[4096,1024]{1,0:T(8,128)(2,1)}) %all-gather.10.cloned.1.call-update) | async-done | bytes 8388624 | tf_op jit(solution)/shard_map/all_gather | solution.py:76
  168.6 14.4 %multiply_add_fusion = f32[1024,1024]{1,0:T(8,128)S(1)} fusion(f32[1024,1024]{1,0:T(8,128)} %param.11, bf16[4096,1024]{1,0:T(8,128)(2,1)} %all-gather.10.cloned.1.call-done, bf16[4096,1024]{1,0:T(8,128)(2,1)} %bitcast.79), kind=kOutput, calls=%fused_computation.4 | convolution fusion | flops 8592031744 | bytes 25165824 | tf_op jit(solution)/shard_map/dot_general | solution.py:75
  183.0 2.0 copy-done.1
  185.0 1.0 fusion.1
  186.3 38.1 %all-gather.14.cloned.1.call-done = f32[16384,20]{0,1:T(8,128)} async-done(((f32[1024,20]{0,1:T(8,128)}), f32[16384,20]{0,1:T(8,128)}) %all-gather.14.cloned.1.call-update) | async-done | bytes 1310736 | tf_op jit(solution)/shard_map/all_gather | solution.py:14
  224.4 2.5 copy.58
  226.9 0.2 bitcast_reduce_fusion.1
  227.1 0.7 fusion.25
  228.0 0.4 reshape.79
  228.5 0.7 broadcast_in_dim.22
  229.2 27.1 %all_to_all.40 = f32[16,1,20880]{2,1,0:T(1,128)S(1)} all-to-all(f32[16,1,20880]{2,1,0:T(1,128)S(1)} %broadcast_in_dim.22), channel_id=1, replica_groups=mesh['row'=16,'col_0'=4,'col_1'=4] {'col_0','col_1'}, dimensions={0} | all-to-all | bytes 2672640 | tf_op jit(solution)/shard_map/all_to_all | solution.py:19
  256.3 0.8 reduce_sum.37
  257.3 1.8 cholesky.59
  259.2 0.6 compare_reduce_fusion.2
  259.8 0.7 fusion.16
  260.5 1.5 custom-call.13
  262.0 0.6 reshape.82
  262.6 0.6 convolution_bitcast_fusion.2
  263.2 3.2 fusion.27
  266.6 15.7 %all-gather.4 = f32[16,20,20]{2,1,0:T(8,128)S(1)} all-gather(f32[1,20,20]{2,1,0:T(8,128)S(1)} %convolution_bitcast_fusion.3), channel_id=4, replica_groups=mesh['row'=16,'col_0'=4,'col_1'=4] {'row'}, dimensions={0}, use_global_device_ids=true | all-gather | bytes 27200 | tf_op jit(solution)/shard_map/all_gather | solution.py:14
  282.4 1.8 cholesky.70
  284.3 0.6 compare_reduce_fusion.1
  284.9 0.7 fusion.15
  285.6 1.5 custom-call.14
  287.1 0.8 gather_fusion.2
  287.9 0.8 gather_fusion.1
  288.7 12.4 %all-gather.16.cloned.1.call-done = f32[16384,20]{0,1:T(8,128)} async-done(((f32[1024,20]{0,1:T(8,128)}), f32[16384,20]{0,1:T(8,128)}) %all-gather.16.cloned.1.call-update) | async-done | bytes 1310736 | tf_op jit(solution)/shard_map/all_gather | solution.py:14
  301.1 2.3 copy.59
  303.4 0.2 bitcast_reduce_fusion
  303.7 0.3 convolution_bitcast_fusion.1
  304.1 16.8 %psum.14 = f32[20,20]{0,1:T(8,128)S(1)} all-reduce(f32[20,20]{0,1:T(8,128)S(1)} %fusion.28), channel_id=1, replica_groups=mesh['row'=16,'col_0'=4,'col_1'=4] {'col_0'}, use_global_device_ids=true, to_apply=%region_6.9 | all-reduce | flops 400 | bytes 3200 | tf_op jit(solution)/shard_map/psum | solution.py:39
  320.9 16.8 %psum.15 = f32[20,20]{0,1:T(8,128)S(1)} all-reduce(f32[20,20]{0,1:T(8,128)S(1)} %psum.14), channel_id=1, replica_groups=mesh['row'=16,'col_0'=4,'col_1'=4] {'col_1'}, use_global_device_ids=true, to_apply=%region_7.10 | all-reduce | flops 400 | bytes 3200 | tf_op jit(solution)/shard_map/psum | solution.py:39
  337.8 1.8 cholesky.81
  339.7 0.6 compare_reduce_fusion
  340.3 0.7 select_bitcast_fusion
  341.0 0.8 gather_fusion.3
  341.8 1.5 custom-call.15
  343.3 1.0 fusion
  344.2 0.6 pad_maximum_fusion.1
  (37 shorter events, 1.6 us)
Async XLA Ops:
  7.2 0.8 copy-start
  7.2 86.3 %all-gather.12.cloned.1.call-start = ((), (), s32[]{:S(2)}) async-start(), calls=%async_computation.4 | async-start | bytes 8912896 | tf_op jit(solution)/shard_map/all_gather | solution.py:73
  30.2 138.4 %all-gather.10.cloned.1.call-start = ((), (), s32[]{:S(2)}) async-start(), calls=%async_computation.3 | async-start | bytes 8912896 | tf_op jit(solution)/shard_map/all_gather | solution.py:76
  55.9 168.6 %all-gather.14.cloned.1.call-start = ((), (), s32[]{:S(2)}) async-start(), calls=%async_computation.5 | async-start | bytes 1671168 | tf_op jit(solution)/shard_map/all_gather | solution.py:14
  168.6 16.4 %copy-start.3 = (f32[1024,20]{0,1:T(8,128)S(1)}, f32[1024,20]{0,1:T(8,128)}, u32[]{:S(2)}) copy-start(f32[1024,20]{0,1:T(8,128)} %param.12) | copy-start | bytes 245764
  183.0 2.0 copy-start.1
  186.1 115.0 %all-gather.16.cloned.1.call-start = ((), (), s32[]{:S(2)}) async-start(), calls=%async_computation.6 | async-start | bytes 1671168 | tf_op jit(solution)/shard_map/all_gather | solution.py:14
  224.4 2.7 copy-start.2
Sparse Core Ops, SparseCore 0:
  30.4 63.0 all-gather.11
  95.9 72.6 all-gather.9
  186.2 38.1 all-gather.13
  266.6 34.5 all-gather.15
where the time goes:
time: 352 us; the launch traced here: 351 us
  waiting for transfers between devices  152 us (43%)
  blocking collectives  120 us (34%)
  local copies, waits for them, and re-layouts  24.6 us (7%)
  matrix products  21.5 us (6%)
  other arithmetic  18.7 us (5%)
  between operations  13.9 us (4%)
    all_gather x1, waiting for transfers between devices, body(): lax.all_gather(row_piece, COL, axis=0, tiled=True)  63.9 us
    all_gather x2, waiting for transfers between devices, total_of_pieces(): return lax.all_gather(array, axis).sum(0)  50.5 us
    all_gather x1, waiting for transfers between devices, body(): col_panel = lax.all_gather(col_piece, 'row', axis=1, tiled=True)  37.5 us
    psum x2, blocking collectives, one_axis_at_a_time(): array = lax.psum(array, axis)  33.6 us
    all_to_all x1, blocking collectives, copy_for_each(): lax.all_to_all(jnp.broadcast_to(array[None], (length, *array.shape)), axi...  27.1 us
    all_to_all x1, blocking collectives, body(): lax.all_to_all(standard, 'row', split_axis=1, concat_axis=0, tiled=True)  25.6 us
    all_to_all x1, blocking collectives, body(): lax.all_to_all(standard, COL, split_axis=1, concat_axis=0, tiled=True)  18.3 us
    all_gather x1, blocking collectives, total_of_pieces(): return lax.all_gather(array, axis).sum(0)  15.7 us
  transfers between devices with their start and end apart: 4, of which 4 were waited for; matrix products, arithmetic and copies ran while one was open for 5% of the time, Pallas kernels for 0%

commit v1 on v0

v1 whole, which is shorter than its diff:
```python
import jax
import jax.numpy as jnp
from jax import lax
from jax.sharding import Mesh
from jax.sharding import PartitionSpec as P

S = 16384
K = 20
ROW = ("z", "core")
COL = ("x", "y")
ALL = ("z", "core", "x", "y")
F32 = jnp.float32


def standardize(genotypes, allele_freq):
    doubled = 2.0 * allele_freq
    spread = jnp.sqrt(doubled * (1.0 - allele_freq))
    return (genotypes.astype(F32) - doubled[:, None]) / spread[:, None]


def bcast_sum(array, axis):
    length = lax.axis_size(axis)
    copies = jnp.broadcast_to(array[None], (length, *array.shape))
    return lax.all_to_all(copies, axis, 0, 0, tiled=True).sum(axis=0)


def swap_core(array):
    return lax.ppermute(array, "core", [(0, 1), (1, 0)])


def with_gram(wide, gram):
    width = wide.shape[1]
    flat = jnp.pad(gram.reshape(4, K * K // 4), ((0, 0), (0, width - K * K // 4)))
    return jnp.concatenate([wide, flat], axis=0)


def split_gram(packed):
    return packed[:K], packed[K:, : K * K // 4].reshape(K, K)


def row_sum(wide, gram=None):
    half = wide.shape[1] // 2
    first = lax.axis_index("core") == 0
    lo, hi = wide[:, :half], wide[:, half:]
    keep, give = jnp.where(first, lo, hi), jnp.where(first, hi, lo)
    if gram is not None:
        keep, give = with_gram(keep, gram), with_gram(give, gram)
    mine = bcast_sum(keep + swap_core(give), "z")
    if gram is not None:
        mine, gram = split_gram(mine)
    other = swap_core(mine)
    full = jnp.where(
        first,
        jnp.concatenate([mine, other], axis=1),
        jnp.concatenate([other, mine], axis=1),
    )
    return full if gram is None else (full, gram)


def col_sum(packed):
    return bcast_sum(bcast_sum(packed, "x"), "y")


def dot_t(a, b, dims):
    return lax.dot_general(a, b, (dims, ((), ())))


def forward(factor, wide):
    return lax.linalg.triangular_solve(factor, wide, left_side=True, lower=True)


def body(genotypes, snp_index, freq_table, prior, start_vectors):
    allele_freq = jnp.take(freq_table, snp_index)
    standard = standardize(genotypes, allele_freq).astype(jnp.bfloat16)
    row_count = lax.axis_size(ROW)
    col_count = lax.axis_size(COL)
    own_snps = genotypes.shape[0]
    total_snps = own_snps * row_count * col_count
    row_piece = lax.all_to_all(standard, ROW, split_axis=1, concat_axis=0, tiled=True)
    col_piece = lax.all_to_all(standard, COL, split_axis=1, concat_axis=0, tiled=True)
    col_piece = col_piece.reshape(col_count, 1, own_snps, col_piece.shape[1])
    col_panel = lax.all_gather(col_piece, ROW, axis=1, tiled=True)
    col_panel = col_panel.reshape(total_snps, col_panel.shape[3])
    window = lax.dot_general(
        lax.all_gather(row_piece, COL, axis=0, tiled=True),
        col_panel,
        (((0,), (0,)), ((), ())),
        preferred_element_type=F32,
    )
    grm = prior + window / total_snps
    start = start_vectors.T / jnp.sqrt(F32(S))
    image = row_sum(dot_t(start, grm, ((1,), (0,))))
    gram1 = dot_t(image, image, ((1,), (1,)))
    packed = with_gram(dot_t(image, grm, ((1,), (1,))), gram1)
    second, gram1 = split_gram(col_sum(packed))
    factor1 = jnp.linalg.cholesky(gram1)
    second = forward(factor1, second)
    third, gram2 = row_sum(
        dot_t(second, grm, ((1,), (0,))), dot_t(second, second, ((1,), (1,)))
    )
    gram3 = bcast_sum(dot_t(third, third, ((1,), (1,))), COL)
    factor2, factor3 = jnp.linalg.cholesky(jnp.stack([gram2, gram3]))
    vectors = forward(factor3, third)
    pcs = vectors.T * jnp.sqrt(F32(S))
    d1, d2, d3 = jnp.diagonal(factor1), jnp.diagonal(factor2), jnp.diagonal(factor3)
    return (grm, pcs, jnp.stack([d1, d2, d3 / d2], axis=0))


def solution(mesh):
    finer = Mesh(mesh.devices.reshape(8, 2, 4, 4), ALL)
    in_specs = (P(ALL, None), P(ALL), P(), P(ROW, COL), P(ROW, None))
    out_specs = (P(ROW, COL), P(COL, None), P())
    return jax.shard_map(body, mesh=finer, in_specs=in_specs, out_specs=out_specs, check_vma=False)
```

time: 352 us -> 296 us (0.84)
  blocking collectives: 120 us -> 87.2 us
  waiting for transfers between devices: 152 us -> 127 us
  starting transfers between devices: 0.35 us -> 8.96 us
  other arithmetic: 18.7 us -> 14.5 us
  local copies, waits for them, and re-layouts: 24.6 us -> 20.7 us
    all_gather x3 -> x1, waiting for transfers between devices: 88 us -> 37.6 us  [body(): col_panel = lax.all_gather(col_piece, ROW, axis=1, tiled=True)]
    psum x2 -> x0, blocking collectives: 33.6 us -> none  [one_axis_at_a_time(): array = lax.psum(array, axis)]
    all_to_all x0 -> x2, waiting for transfers between devices: none -> 20.4 us  [bcast_sum(): return lax.all_to_all(copies, axis, 0, 0, tiled=True).sum(axis=0)]
    all_to_all x2 -> x4, blocking collectives: 52.6 us -> 68.9 us  [the longest x3 43.3 us: bcast_sum(): return lax.all_to_all(copies, axis, 0, 0, tiled=True).sum(axis=0)]
    all_gather x1 -> x0, blocking collectives: 15.7 us -> none  [total_of_pieces(): return lax.all_gather(array, axis).sum(0)]
    all_to_all x0 -> x2, starting transfers between devices: none -> 8.33 us  [bcast_sum(): return lax.all_to_all(copies, axis, 0, 0, tiled=True).sum(axis=0)]
    ppermute x0 -> x4, waiting for transfers between devices: none -> 4.82 us  [swap_core(): return lax.ppermute(array, 'core', [(0, 1), (1, 0)])]
    another operation x16 -> x14, other arithmetic: 14.6 us -> 10.7 us  [the longest x5 3.83 us: body(): factor2, factor3 = jnp.linalg.cholesky(jnp.stack([gram2, gram3]))]
  transfers between devices with their start and end apart: 4 -> 8, of which waited for: 4 -> 8; matrix products, arithmetic and copies ran while one was open for 5% -> 4% of each run, Pallas kernels for 0% -> 0%
where the time goes in v1:
time: 296 us; the launch traced here: 294 us
  waiting for transfers between devices  127 us (43%)
  blocking collectives  87.2 us (29%)
  matrix products  21.8 us (7%)
  local copies, waits for them, and re-layouts  20.7 us (7%)
  other arithmetic  14.5 us (5%)
  between operations  14.3 us (5%)
  starting transfers between devices  8.96 us (3%)
    all_gather x1, waiting for transfers between devices, body(): lax.all_gather(row_piece, COL, axis=0, tiled=True)  63.9 us
    all_to_all x3, blocking collectives, bcast_sum(): return lax.all_to_all(copies, axis, 0, 0, tiled=True).sum(axis=0)  43.3 us
    all_gather x1, waiting for transfers between devices, body(): col_panel = lax.all_gather(col_piece, ROW, axis=1, tiled=True)  37.6 us
    all_to_all x1, blocking collectives, body(): lax.all_to_all(standard, ROW, split_axis=1, concat_axis=0, tiled=True)  25.6 us
    all_to_all x2, waiting for transfers between devices, bcast_sum(): return lax.all_to_all(copies, axis, 0, 0, tiled=True).sum(axis=0)  20.4 us
    all_to_all x1, blocking collectives, body(): lax.all_to_all(standard, COL, split_axis=1, concat_axis=0, tiled=True)  18.3 us
    dot_general x1, matrix products, body(): lax.dot_general(lax.all_gather(row_piece, COL, axis=0, tiled=True), col_p...  14.4 us
    all_gather x1, local copies, waits for them, and re-layouts, body(): col_panel = lax.all_gather(col_piece, ROW, axis=1, tiled=True)  11.3 us
  transfers between devices with their start and end apart: 8, of which 8 were waited for; matrix products, arithmetic and copies ran while one was open for 4% of the time, Pallas kernels for 0%

profile of v1, /device:TPU:32, one launch (start us, length us, event | category | flops | bytes accessed | tf_op | source)
XLA Modules:
  0.0 294.1 jit_solution(18259528890697440130)
XLA Ops:
  7.2 0.7 compare_select_fusion
  7.9 0.1 copy-done
  8.0 0.7 gather_fusion
  8.7 0.7 broadcast_multiply_fusion
  9.3 1.4 divide_convert_fusion
  10.8 18.3 %all_to_all.57 = bf16[16,16,1024]{2,0,1:T(8,128)(2,1)S(1)} all-to-all(bf16[16,16,1024]{2,0,1:T(8,128)(2,1)S(1)} %bitcast.53), channel_id=1, replica_groups=mesh['z'=8,'core'=2,'x'=4,'y'=4] {'x','y'}, dimensions={1} | all-to-all | bytes 1048576 | tf_op jit(solution)/shard_map/all_to_all | solution.py:80
  29.1 1.1 copy.35
  30.3 25.6 %all_to_all.58 = bf16[16,16,1024]{2,0,1:T(8,128)(2,1)} all-to-all(bf16[16,16,1024]{2,0,1:T(8,128)(2,1)S(1)} %bitcast.54), channel_id=1, replica_groups=mesh['z'=8,'core'=2,'x'=4,'y'=4] {'z','core'}, dimensions={1} | all-to-all | bytes 1048576 | tf_op jit(solution)/shard_map/all_to_all | solution.py:79
  55.9 37.6 %all-gather.6.cloned.1.call-done = bf16[16,256,1024]{2,0,1:T(8,128)(2,1)} async-done(((bf16[16,16,1024]{2,0,1:T(8,128)(2,1)}), bf16[16,256,1024]{2,0,1:T(8,128)(2,1)}) %all-gather.6.cloned.1.call-update) | async-done | bytes 8388624 | tf_op jit(solution)/shard_map/all_gather | solution.py:82
  93.5 11.3 %copy.36 = bf16[16,256,1024]{2,1,0:T(8,128)(2,1)} copy(bf16[16,256,1024]{2,0,1:T(8,128)(2,1)} %all-gather.6.cloned.1.call-done) | data formatting | bytes 16777216 | tf_op jit(solution)/shard_map/all_gather | solution.py:82
  104.8 63.9 %all-gather.4.cloned.1.call-done = bf16[4096,1024]{1,0:T(8,128)(2,1)} async-done(((bf16[256,1024]{1,0:T(8,128)(2,1)}), bf16[4096,1024]{1,0:T(8,128)(2,1)}) %all-gather.4.cloned.1.call-update) | async-done | bytes 8388624 | tf_op jit(solution)/shard_map/all_gather | solution.py:85
  168.6 14.4 %multiply_add_fusion = f32[1024,1024]{1,0:T(8,128)S(1)} fusion(f32[1024,1024]{1,0:T(8,128)} %param.10, bf16[4096,1024]{1,0:T(8,128)(2,1)} %all-gather.4.cloned.1.call-done, bf16[4096,1024]{1,0:T(8,128)(2,1)} %bitcast.52), kind=kOutput, calls=%fused_computation.4 | convolution fusion | flops 8592031744 | bytes 25165824 | tf_op jit(solution)/shard_map/dot_general | solution.py:84
  183.0 2.0 copy-done.1
  185.0 0.4 fusion.3
  185.5 1.2 collective-permute-done
  186.8 20.8 %all_to_all.59 = f32[8,20,512]{2,1,0:T(8,128)S(1)} all-to-all(f32[8,20,512]{2,1,0:T(8,128)S(1)} %broadcast_in_dim.30), channel_id=1, replica_groups=mesh['z'=8,'core'=2,'x'=4,'y'=4] {'z'}, dimensions={0} | all-to-all | bytes 655360 | tf_op jit(solution)/shard_map/all_to_all | solution.py:24
  207.7 0.3 collective-permute-start.1
  208.0 1.2 collective-permute-done.1
  209.1 0.1 fusion.6
  209.3 2.9 fusion.7
  212.3 12.4 %all_to_all.60 = f32[4,24,1024]{2,1,0:T(8,128)S(1)} all-to-all(f32[4,24,1024]{2,1,0:T(8,128)S(1)} %broadcast_in_dim.31), channel_id=1, replica_groups=mesh['z'=8,'core'=2,'x'=4,'y'=4] {'x'}, dimensions={0} | all-to-all | bytes 786432 | tf_op jit(solution)/shard_map/all_to_all | solution.py:24
  224.8 10.0 %all_to_all.61 = f32[4,24,1024]{2,1,0:T(8,128)S(1)} all-to-all(f32[4,24,1024]{2,1,0:T(8,128)S(1)} %broadcast_in_dim.56), channel_id=1, replica_groups=mesh['z'=8,'core'=2,'x'=4,'y'=4] {'y'}, dimensions={0} | all-to-all | bytes 786432 | tf_op jit(solution)/shard_map/all_to_all | solution.py:24
  235.0 1.8 cholesky.35
  236.9 0.6 compare_reduce_fusion.1
  237.5 0.7 select_bitcast_fusion.1
  238.2 1.5 custom-call.18
  239.7 0.3 fusion.1
  240.0 2.6 fusion.25
  242.6 0.1 fusion.26
  243.0 1.2 collective-permute-done.2
  244.2 0.8 broadcast_in_dim.57
  245.0 4.8 %all-to-all-start.5 = ((f32[8,24,512]{2,1,0:T(8,128)}), f32[8,24,512]{2,1,0:T(8,128)S(1)}, u32[]{:S(2)}, u32[]{:S(2)}) async-start(f32[8,24,512]{2,1,0:T(8,128)} %broadcast_in_dim.57), calls=%async_computation.5 | async-start | bytes 786432 | tf_op jit(solution)/shard_map/all_to_all | solution.py:24
  249.8 13.9 %all-to-all-done.5 = f32[8,24,512]{2,1,0:T(8,128)S(1)} async-done(((f32[8,24,512]{2,1,0:T(8,128)}), f32[8,24,512]{2,1,0:T(8,128)S(1)}, u32[]{:S(2)}, u32[]{:S(2)}) %all-to-all-start.5) | async-done | bytes 393248 | tf_op jit(solution)/shard_map/all_to_all | solution.py:24
  263.8 1.2 collective-permute-done.3
  265.0 0.1 fusion.5
  265.2 0.8 reshape.115
  266.0 3.5 %all-to-all-start.6 = ((f32[16,1,400]{2,1,0:T(1,128)}), f32[16,1,400]{2,1,0:T(1,128)S(1)}, u32[]{:S(2)}, u32[]{:S(2)}) async-start(f32[16,1,400]{2,1,0:T(1,128)} %reshape.115), calls=%async_computation.6 | async-start | bytes 65536 | tf_op jit(solution)/shard_map/all_to_all | solution.py:24
  269.6 0.8 gather_fusion.1
  270.5 6.6 %all-to-all-done.6 = f32[16,1,400]{2,1,0:T(1,128)S(1)} async-done(((f32[16,1,400]{2,1,0:T(1,128)}), f32[16,1,400]{2,1,0:T(1,128)S(1)}, u32[]{:S(2)}, u32[]{:S(2)}) %all-to-all-start.6) | async-done | bytes 25632 | tf_op jit(solution)/shard_map/all_to_all | solution.py:24
  277.1 0.5 broadcast.195
  277.6 0.7 reduce.12
  278.7 3.7 %custom-call.10 = f32[2,20,20]{2,1,0:T(8,128)S(1)} custom-call(f32[2,20,20]{2,1,0:T(8,128)S(1)} %fusion.16), custom_call_target="Cholesky" | custom-call | tf_op jit(solution)/shard_map/jit(cholesky)/cholesky | solution.py:102
  282.4 0.1 compare_reduce_fusion
  282.6 0.8 gather_fusion.2
  283.4 0.8 gather_fusion.3
  284.2 1.5 custom-call.19
  285.7 0.6 pad_maximum_fusion.1
  286.4 0.9 fusion
  (52 shorter events, 1.8 us)
Async XLA Ops:
  7.2 0.8 copy-start
  7.2 86.3 %all-gather.6.cloned.1.call-start = ((), (), s32[]{:S(2)}) async-start(), calls=%async_computation.8 | async-start | bytes 8912896 | tf_op jit(solution)/shard_map/all_gather | solution.py:82
  30.2 138.4 %all-gather.4.cloned.1.call-start = ((), (), s32[]{:S(2)}) async-start(), calls=%async_computation.7 | async-start | bytes 8912896 | tf_op jit(solution)/shard_map/all_gather | solution.py:85
  168.6 16.4 %copy-start.2 = (f32[1024,20]{0,1:T(8,128)S(1)}, f32[1024,20]{0,1:T(8,128)}, u32[]{:S(2)}) copy-start(f32[1024,20]{0,1:T(8,128)} %param.11) | copy-start | bytes 245764
  183.0 2.0 copy-start.1
  185.4 1.3 collective-permute-start
  207.7 1.5 collective-permute-start.1
  242.9 1.3 collective-permute-start.2
  245.0 18.7 %all-to-all-start.5 = ((f32[8,24,512]{2,1,0:T(8,128)}), f32[8,24,512]{2,1,0:T(8,128)S(1)}, u32[]{:S(2)}, u32[]{:S(2)}) async-start(f32[8,24,512]{2,1,0:T(8,128)} %broadcast_in_dim.57), calls=%async_computation.5 | async-start | bytes 786432 | tf_op jit(solution)/shard_map/all_to_all | solution.py:24
  263.7 1.3 collective-permute-start.3
  266.0 11.1 %all-to-all-start.6 = ((f32[16,1,400]{2,1,0:T(1,128)}), f32[16,1,400]{2,1,0:T(1,128)S(1)}, u32[]{:S(2)}, u32[]{:S(2)}) async-start(f32[16,1,400]{2,1,0:T(1,128)} %reshape.115), calls=%async_computation.6 | async-start | bytes 65536 | tf_op jit(solution)/shard_map/all_to_all | solution.py:24
Sparse Core Ops, SparseCore 0:
  30.4 63.0 all-gather.5
  95.9 72.6 all-gather.3
